TPU v7x, 32 devices: a whole 2x2x4 slice. The times are simulated.
32 devices in a mesh: dp: 4 (over z), expert: 8 (over y, x, core).
Axes of the slice: x: 2, y: 2, z: 4, core: 2. Of those that a mesh axis runs over, the one named last changes fastest.
Arguments:
- tokens: bfloat16 [32, 212, 1024], P(('dp', 'expert')), may hold values from -6 to 6
- expert_ids: int32 [32, 212, 1], P(('dp', 'expert')), may hold values from 0 to 7; in each aligned block of 212 rows (0 to 211, 212 to 423, ..., all dimensions but the last counted through in order) at most 36 rows name the same one
- caption_lengths: int32 [32], P(('dp', 'expert')), may hold values from 1 to 16, as said below
- layer_norm_gain: float32 [1024], replicated, may hold values from 0.5 to 1.5
- router: float32 [1024, 8], replicated, may hold values from -0.1875 to 0.1875
- w_up: bfloat16 [8, 1024, 4096], P('expert', None, 'dp'), may hold values from -0.1875 to 0.1875
- w_down: bfloat16 [8, 4096, 1024], P('expert', 'dp'), may hold values from -0.09375 to 0.09375
- logit_scale: float32 [1], replicated, may hold values from 5 to 20
- logit_bias: float32 [1], replicated, may hold values from -4 to -1.5
Outputs:
- loss: float32 [1], replicated
- grad_tokens: bfloat16 [32, 212, 1024], P(('dp', 'expert'))
- grad_up: float32 [8, 1024, 4096], P('expert', None, 'dp')
- grad_down: float32 [8, 4096, 1024], P('expert', 'dp')
- grad_router: float32 [1024, 8], replicated
- layer_gain_gradient: float32 [1024], replicated
Inputs may be any that keep to these rules, and one draw needn't show every extreme that they name: `expert_ids`: among the rows of one device (aligned blocks of 212 rows, devices ordered by dp then expert) no expert is named more than 36 times, a bound that some block reaches. `caption_lengths`: some caption has all 16 tokens.
All inputs are finite; a program needn't handle non-finite values.
Results may differ from a plain program's by a relative error of at most 0.009.
Values may be sent and summed in bfloat16 or wider, within the bound.
A program may use at most 128 MiB of HBM per device.

v0:
```python
import jax
import jax.numpy as jnp
from jax import lax
from jax.sharding import PartitionSpec as P

D = 1024
PATCH = 196
CAPLEN = 16
SEQ = 212
eps = 1e-06
loss_scale = 1024.0


def gelu_slope(pre):
    return (
        0.5 * (1.0 + lax.erf(pre * 0.7071067811865476))
        + pre * jnp.exp(-0.5 * pre * pre) * 0.3989422804014327
    )


def deliver(buffer, experts, slots):
    width = buffer.shape[-1]
    sent = lax.all_to_all(
        buffer.reshape(experts, 1, slots, width), "expert", split_axis=0, concat_axis=1, tiled=True
    )
    shaped = sent.reshape(sent.shape[0], 1, sent.shape[1], slots, width)
    whole = lax.all_gather(shaped, "dp", axis=1, tiled=True)
    return whole.reshape(whole.shape[0], -1, width)


def give_back(partial_value, n_dp, n_expert, slots):
    local = partial_value.shape[0]
    width = partial_value.shape[-1]
    summed = lax.psum_scatter(
        partial_value.reshape(local, n_dp, n_expert * slots, width).astype(jnp.bfloat16),
        "dp",
        scatter_dimension=1,
        tiled=True,
    )
    rounded = summed.reshape(local, n_expert, slots, width)
    returned = lax.all_to_all(rounded, "expert", split_axis=1, concat_axis=0, tiled=True)
    return returned.reshape(-1, width)


def body(
    tokens,
    expert_ids,
    caption_lengths,
    layer_norm_gain,
    router,
    w_up,
    w_down,
    logit_scale,
    logit_bias,
):
    n_dp = lax.axis_size("dp")
    n_expert = lax.axis_size("expert")
    pair_dev = tokens.shape[0]
    rows = pair_dev * SEQ
    experts = router.shape[1]
    slots = rows * 4 // (3 * experts) + 1
    pairs_all = pair_dev * n_dp * n_expert
    input_rows = tokens.reshape(rows, D).astype(jnp.float32)
    input_mean = jnp.mean(input_rows, axis=1, keepdims=True)
    var_x = jnp.mean((input_rows - input_mean) ** 2, axis=1, keepdims=True)
    inverse_deviation = 1.0 / jnp.sqrt(var_x + eps)
    centered_scaled_input = (input_rows - input_mean) * inverse_deviation
    normalized_input = (centered_scaled_input * layer_norm_gain).astype(jnp.bfloat16)
    ids = expert_ids.reshape(rows)
    onehot = (ids[:, None] == jnp.arange(experts, dtype=jnp.int32)[None, :]).astype(jnp.int32)
    slot = jnp.sum((jnp.cumsum(onehot, axis=0) - 1) * onehot, axis=1)
    dest = ids * slots + slot
    onehot_f = onehot.astype(jnp.float32)
    buffer = jnp.zeros((experts * slots, D), jnp.bfloat16).at[dest].set(normalized_input)
    gathered = deliver(buffer, experts, slots)
    pre = jnp.einsum("erd,edf->erf", gathered, w_up, preferred_element_type=jnp.float32)
    act = jax.nn.gelu(pre, approximate=False).astype(jnp.bfloat16)
    partial_value = jnp.einsum("erf,efd->erd", act, w_down, preferred_element_type=jnp.float32)
    moe = give_back(partial_value, n_dp, n_expert, slots)[dest].astype(jnp.float32)
    xnf = normalized_input.astype(jnp.float32)
    router_logits = jnp.dot(xnf, router, precision=lax.Precision.HIGHEST)
    gate = jax.nn.sigmoid(jnp.sum(router_logits * onehot_f, axis=1))
    y = (input_rows + gate[:, None] * moe).reshape(pair_dev, SEQ, D)
    img = jnp.mean(y[:, :PATCH], axis=1)
    lengths = caption_lengths.astype(jnp.float32)
    mask = (jnp.arange(CAPLEN, dtype=jnp.int32)[None, :] < caption_lengths[:, None]).astype(
        jnp.float32
    )
    txt = jnp.sum(y[:, PATCH:] * mask[:, :, None], axis=1) / lengths[:, None]
    ru = jnp.sqrt(jnp.mean(img * img, axis=1, keepdims=True) + eps)
    rv = jnp.sqrt(jnp.mean(txt * txt, axis=1, keepdims=True) + eps)
    u = img / ru
    v = txt / rv
    scale = logit_scale[0]
    first = lax.axis_index(("dp", "expert")) * pair_dev
    mine = first + jnp.arange(pair_dev, dtype=jnp.int32)
    every = jnp.arange(pairs_all, dtype=jnp.int32)
    own_sign = jnp.where(mine[:, None] == every[None, :], 1.0, -1.0)
    u_all, v_all = (
        lax.all_gather(u, ("dp", "expert"), axis=0, tiled=True),
        lax.all_gather(v, ("dp", "expert"), axis=0, tiled=True),
    )
    logits = scale * jnp.dot(u, v_all.T, precision=lax.Precision.HIGHEST) / D + logit_bias[0]
    loss_term = -jnp.sum(jax.nn.log_sigmoid(own_sign * logits)) / pairs_all
    coef = -(loss_scale / pairs_all) * own_sign * jax.nn.sigmoid(-own_sign * logits)
    du = scale / D * jnp.dot(coef, v_all, precision=lax.Precision.HIGHEST)
    column_logits = scale * jnp.dot(u_all, v.T, precision=lax.Precision.HIGHEST) / D + logit_bias[0]
    column_sign = own_sign.T
    column_coef = (
        -(loss_scale / pairs_all) * column_sign * jax.nn.sigmoid(-column_sign * column_logits)
    )
    dv = scale / D * jnp.dot(column_coef.T, u_all, precision=lax.Precision.HIGHEST)
    dimg = (du - u * jnp.mean(du * u, axis=1, keepdims=True)) / ru
    dtxt = (dv - v * jnp.mean(dv * v, axis=1, keepdims=True)) / rv
    dy_img = jnp.broadcast_to(dimg[:, None, :] / PATCH, (pair_dev, PATCH, D))
    dy_txt = (dtxt / lengths[:, None])[:, None, :] * mask[:, :, None]
    dy = jnp.concatenate([dy_img, dy_txt], axis=1).reshape(rows, D)
    dmoe = (gate[:, None] * dy).astype(jnp.bfloat16)
    dgl = jnp.sum(dy * moe, axis=1) * gate * (1.0 - gate)
    router_part = jnp.dot(xnf.T, onehot_f * dgl[:, None], precision=lax.Precision.HIGHEST)
    grad_buffer = jnp.zeros((experts * slots, D), jnp.bfloat16).at[dest].set(dmoe)
    gathered_grads = deliver(grad_buffer, experts, slots)
    dact = jnp.einsum("erd,efd->erf", gathered_grads, w_down, preferred_element_type=jnp.float32)
    dpre = (dact * gelu_slope(pre)).astype(jnp.bfloat16)
    grad_down = jnp.einsum("erf,erd->efd", act, gathered_grads, preferred_element_type=jnp.float32)
    grad_up = jnp.einsum("erd,erf->edf", gathered, dpre, preferred_element_type=jnp.float32)
    back_partial = jnp.einsum("erf,edf->erd", dpre, w_up, preferred_element_type=jnp.float32)
    dxe = give_back(back_partial, n_dp, n_expert, slots)[dest].astype(jnp.float32)
    router_rows = jnp.dot(onehot_f, router.T, precision=lax.Precision.HIGHEST)
    gradient_normalized_input = dxe + dgl[:, None] * router_rows
    gain_partial_term = jnp.sum(gradient_normalized_input * centered_scaled_input, axis=0)
    scaled_output_gradient = gradient_normalized_input * layer_norm_gain
    normed_input_gradient = (
        scaled_output_gradient
        - jnp.mean(scaled_output_gradient, axis=1, keepdims=True)
        - centered_scaled_input
        * jnp.mean(scaled_output_gradient * centered_scaled_input, axis=1, keepdims=True)
    ) * inverse_deviation
    grad_tokens = (dy + normed_input_gradient).astype(jnp.bfloat16).reshape(pair_dev, SEQ, D)
    loss, grad_router, layer_gain_gradient = lax.psum(
        (loss_term, router_part, gain_partial_term), ("dp", "expert")
    )
    return (loss.reshape(1), grad_tokens, grad_up, grad_down, grad_router, layer_gain_gradient)


def solution(mesh):
    return jax.shard_map(
        body,
        mesh=mesh,
        in_specs=(
            P(("dp", "expert"), None, None),
            P(("dp", "expert"), None, None),
            P(("dp", "expert")),
            P(),
            P(),
            P("expert", None, "dp"),
            P("expert", "dp", None),
            P(),
            P(),
        ),
        out_specs=(
            P(),
            P(("dp", "expert"), None, None),
            P("expert", None, "dp"),
            P("expert", "dp", None),
            P(),
            P(),
        ),
        check_vma=False,
    )
```

profile of v0, /device:TPU:0, one launch (start us, length us, event | category | flops | bytes accessed | tf_op | source)
XLA Modules:
  0.0 468.2 jit_solution(15633228378693927035)
XLA Ops:
  15.3 16.1 %all_to_all.16 = bf16[8,1,36,1024]{3,2,1,0:T(8,128)(2,1)S(1)} all-to-all(bf16[8,1,36,1024]{3,2,1,0:T(8,128)(2,1)S(1)} %bitcast.185), channel_id=1, replica_groups=mesh['dp'=4,'expert'=8] {'expert'}, dimensions={0} | all-to-all | bytes 1179648 | tf_op jit(solution)/shard_map/all_to_all | solution.py:23
  32.6 49.5 %all-gather.7.cloned.1.call-done = bf16[32,1,36,1024]{3,0,2,1:T(8,128)(2,1)} async-done(((bf16[8,1,36,1024]{3,0,2,1:T(8,128)(2,1)}), bf16[32,1,36,1024]{3,0,2,1:T(8,128)(2,1)}) %all-gather.7.cloned.1.call-update) | async-done | bytes 2359312 | tf_op jit(solution)/shard_map/all_gather | solution.py:27
  82.1 4.5 copy.17
  86.5 4.1 reshape.516
  90.7 14.6 %fusion.2 = (bf16[1152,1024]{1,0:T(8,128)(2,1)S(1)}, f32[1152,1024]{1,0:T(8,128)}) fusion(bf16[1152,1024]{1,0:T(8,128)(2,1)} %reshape.516, bf16[1,1024,1024]{2,1,0:T(8,128)(2,1)S(1)} %copy-done), kind=kOutput, calls=%fused_computation.9 | convolution fusion | flops 2492596224 | bytes 11534336 | tf_op jit(solution)/shard_map/erd,edf->erf/dot_general | solution.py:76
  106.7 3.8 convert_bitcast_fusion.1
  111.5 45.7 %reduce-scatter.3.cloned.1.call-done = bf16[1,1,288,1024]{3,2,1,0:T(8,128)(2,1)} async-done(((bf16[1,4,288,1024]{3,2,1,0:T(8,128)(2,1)}), bf16[1,1,288,1024]{3,2,1,0:T(8,128)(2,1)}) %reduce-scatter.3.cloned.1.call-update) | async-done | bytes 589840 | tf_op jit(solution)/shard_map/reduce_scatter | solution.py:34
  159.2 4.2 all-to-all-start.1
  165.3 9.2 %all-to-all-done.1 = bf16[1,8,36,1024]{3,2,0,1:T(8,128)(2,1)} async-done(((bf16[1,8,36,1024]{3,2,0,1:T(8,128)(2,1)}), bf16[1,8,36,1024]{3,2,0,1:T(8,128)(2,1)}, u32[]{:S(2)}, u32[]{:S(2)}) %all-to-all-start.1) | async-done | bytes 589856 | tf_op jit(solution)/shard_map/all_to_all | solution.py:41
  181.6 38.6 %all-gather.1 = f32[32768]{0:T(1024)S(1)} all-gather(f32[1024]{0:T(1024)S(1)} %broadcast_divide_fusion), channel_id=3, replica_groups=mesh['dp'=4,'expert'=8] {'dp','expert'}, dimensions={0}, use_global_device_ids=true | all-gather | bytes 135168 | tf_op jit(solution)/shard_map/all_gather | solution.py:101
  220.2 37.2 %all-gather.2 = f32[32768]{0:T(1024)S(1)} all-gather(f32[1024]{0:T(1024)S(1)} %multiply_divide_fusion), channel_id=4, replica_groups=mesh['dp'=4,'expert'=8] {'dp','expert'}, dimensions={0}, use_global_device_ids=true | all-gather | bytes 135168 | tf_op jit(solution)/shard_map/all_gather | solution.py:100
  266.0 14.6 %all_to_all.17 = bf16[8,1,36,1024]{3,2,1,0:T(8,128)(2,1)S(1)} all-to-all(bf16[8,1,36,1024]{3,2,1,0:T(8,128)(2,1)} %bitcast.186), channel_id=1, replica_groups=mesh['dp'=4,'expert'=8] {'expert'}, dimensions={0} | all-to-all | bytes 1179648 | tf_op jit(solution)/shard_map/all_to_all | solution.py:23
  281.8 46.4 %all-gather.9.cloned.1.call-done = bf16[32,1,36,1024]{3,0,2,1:T(8,128)(2,1)} async-done(((bf16[8,1,36,1024]{3,0,2,1:T(8,128)(2,1)}), bf16[32,1,36,1024]{3,0,2,1:T(8,128)(2,1)}) %all-gather.9.cloned.1.call-update) | async-done | bytes 2359312 | tf_op jit(solution)/shard_map/all_gather | solution.py:27
  328.2 4.5 copy.21
  332.7 4.1 reshape.525
  336.8 6.8 %fusion.14 = bf16[1152,1024]{1,0:T(8,128)(2,1)S(1)} fusion(f32[1152,1024]{1,0:T(8,128)} %get-tuple-element.13, bf16[1152,1024]{1,0:T(8,128)(2,1)} %reshape.525, bf16[1,1024,1024]{2,1,0:T(8,128)(2,1)} %param.15), kind=kOutput, calls=%fused_computation.29 | convolution fusion | flops 2427715584 | bytes 11534336 | tf_op jit(solution)/shard_map/erd,efd->erf/dot_general | solution.py:123
  345.0 3.9 convert_bitcast_fusion
  352.2 7.7 %convolution_bitcast_fusion = f32[1,1024,1024]{2,1,0:T(8,128)} fusion(bf16[1152,1024]{1,0:T(8,128)(2,1)} %copy-done.8, bf16[1152,1024]{1,0:T(8,128)(2,1)} %reshape.525), kind=kOutput, calls=%fused_computation.32 | convolution fusion | flops 2415919104 | bytes 8912896 | tf_op jit(solution)/shard_map/erf,erd->efd/dot_general | solution.py:125
  359.9 35.7 %reduce-scatter.5.cloned.1.call-done = bf16[1,1,288,1024]{3,2,1,0:T(8,128)(2,1)} async-done(((bf16[1,4,288,1024]{3,2,1,0:T(8,128)(2,1)}), bf16[1,1,288,1024]{3,2,1,0:T(8,128)(2,1)}) %reduce-scatter.5.cloned.1.call-update) | async-done | bytes 589840 | tf_op jit(solution)/shard_map/reduce_scatter | solution.py:34
  397.6 4.4 all-to-all-start.3
  402.0 7.3 %convolution_bitcast_fusion.1 = f32[1,1024,1024]{2,1,0:T(8,128)} fusion(bf16[1152,1024]{1,0:T(8,128)(2,1)} %reshape.516, bf16[1152,1024]{1,0:T(8,128)(2,1)} %copy-done.9), kind=kOutput, calls=%fused_computation.33 | convolution fusion | flops 2415919104 | bytes 8912896 | tf_op jit(solution)/shard_map/erd,erf->edf/dot_general | solution.py:126
  409.4 3.6 all-to-all-done.3
  416.0 3.1 fusion.56
  419.1 40.1 %all-reduce.1 = (f32[1]{0:T(128)}, f32[1024,8]{0,1:T(8,128)}, f32[1024]{0:T(1024)}) all-reduce(f32[1]{0:T(128)} %bitcast.22, f32[1024,8]{0,1:T(8,128)S(1)} %fusion.70, f32[1024]{0:T(1024)S(1)} %get-tuple-element.6), channel_id=1, replica_groups=mesh['dp'=4,'expert'=8] {'dp','expert'}, use_global_device_ids=true, to_apply=%region_13.14 | all-reduce | flops 9217 | bytes 73736 | tf_op jit(solution)/shard_map/psum | solution.py:140
  (82 shorter events, 39.1 us)
Async XLA Ops:
  7.2 83.5 %copy-start = (bf16[1,1024,1024]{2,1,0:T(8,128)(2,1)S(1)}, bf16[1,1024,1024]{2,1,0:T(8,128)(2,1)}, u32[]{:S(2)}) copy-start(bf16[1,1024,1024]{2,1,0:T(8,128)(2,1)} %param.14) | copy-start | bytes 6291460
  7.2 74.9 %all-gather.7.cloned.1.call-start = ((), (), s32[]{:S(2)}) async-start(), calls=%async_computation.8 | async-start | bytes 2949120 | tf_op jit(solution)/shard_map/all_gather | solution.py:27
  32.6 124.7 %reduce-scatter.3.cloned.1.call-start = ((), (), s32[]{:S(2)}) async-start(), calls=%async_computation.6 | async-start | bytes 2949120 | tf_op jit(solution)/shard_map/reduce_scatter | solution.py:34
  90.6 16.1 %copy-start.7 = (bf16[1,1024,1024]{2,1,0:T(8,128)(2,1)S(1)}, bf16[1,1024,1024]{2,1,0:T(8,128)(2,1)}, u32[]{:S(2)}) copy-start(bf16[1,1024,1024]{2,1,0:T(8,128)(2,1)} %param.15) | copy-start | bytes 6291460
  105.3 1.5 copy-start.8
  106.7 4.5 copy-start.1
  106.7 4.5 copy-start.4
  110.6 54.3 %copy-start.5 = (f32[1024,8]{0,1:T(8,128)S(1)}, f32[1024,8]{0,1:T(8,128)}, u32[]{:S(2)}) copy-start(f32[1024,8]{0,1:T(8,128)} %param.13) | copy-start | bytes 98308
  110.6 54.3 %copy-start.6 = (s32[1,212,1]{1,2,0:T(1,128)S(1)}, s32[1,212,1]{1,2,0:T(1,128)}, u32[]{:S(2)}) copy-start(s32[1,212,1]{1,2,0:T(1,128)} %param.10) | copy-start | bytes 2548
  111.5 53.8 %copy-start.3 = (bf16[212,1024]{1,0:T(8,128)(2,1)}, bf16[212,1024]{1,0:T(8,128)(2,1)S(1)}, u32[]{:S(2)}) copy-start(bf16[212,1024]{1,0:T(8,128)(2,1)S(1)} %fusion.50) | copy-start | bytes 1302532
  159.2 15.3 %all-to-all-start.1 = ((bf16[1,8,36,1024]{3,2,0,1:T(8,128)(2,1)}), bf16[1,8,36,1024]{3,2,0,1:T(8,128)(2,1)}, u32[]{:S(2)}, u32[]{:S(2)}) async-start(bf16[1,8,36,1024]{3,2,0,1:T(8,128)(2,1)} %bitcast.184), calls=%async_computation.2 | async-start | bytes 1310720 | tf_op jit(solution)/shard_map/all_to_all | solution.py:41
  163.4 164.8 %all-gather.9.cloned.1.call-start = ((), (), s32[]{:S(2)}) async-start(), calls=%async_computation.9 | async-start | bytes 2949120 | tf_op jit(solution)/shard_map/all_gather | solution.py:27
  261.6 88.0 %copy-start.2 = (f32[1,196,1024]{2,1,0:T(8,128)}, f32[1,196,1024]{2,1,0:T(8,128)S(1)}, u32[]{:S(2)}) copy-start(f32[1,196,1024]{2,1,0:T(8,128)S(1)} %broadcast_in_dim.10) | copy-start | bytes 2408452
  281.8 113.9 %reduce-scatter.5.cloned.1.call-start = ((), (), s32[]{:S(2)}) async-start(), calls=%async_computation.7 | async-start | bytes 2949120 | tf_op jit(solution)/shard_map/reduce_scatter | solution.py:34
  343.6 1.4 copy-start.9
  397.6 15.3 %all-to-all-start.3 = ((bf16[1,8,36,1024]{3,2,0,1:T(8,128)(2,1)}), bf16[1,8,36,1024]{3,2,0,1:T(8,128)(2,1)}, u32[]{:S(2)}, u32[]{:S(2)}) async-start(bf16[1,8,36,1024]{3,2,0,1:T(8,128)(2,1)} %bitcast.34), calls=%async_computation.5 | async-start | bytes 1310720 | tf_op jit(solution)/shard_map/all_to_all | solution.py:41
Sparse Core Ops, SparseCore 0:
  32.7 49.3 all-gather.6
  110.7 46.4 reduce-scatter.2
  281.9 46.2 all-gather.8
  349.1 46.4 reduce-scatter.4
where the time goes:
time: 470 us; the launch traced here: 468 us
  waiting for transfers between devices  190 us (40%)
  blocking collectives  147 us (31%)
  matrix products  50.6 us (11%)
  local copies, waits for them, and re-layouts  34.9 us (7%)
  between operations  19.4 us (4%)
  other arithmetic  18 us (4%)
  starting transfers between devices  8.79 us (2%)
    all_gather x2, waiting for transfers between devices, deliver(): whole = lax.all_gather(shaped, 'dp', axis=1, tiled=True)  95.9 us
    reduce_scatter x2, waiting for transfers between devices, give_back(): lax.psum_scatter(partial_value.reshape(local, n_dp, n_expert * slots, wid...  81.4 us
    psum x1, blocking collectives, body(): lax.psum((loss_term, router_part, gain_partial_term), ('dp', 'expert'))  40.1 us
    all_gather x1, blocking collectives, body(): lax.all_gather(v, ('dp', 'expert'), axis=0, tiled=True)  38.6 us
    all_gather x1, blocking collectives, body(): lax.all_gather(u, ('dp', 'expert'), axis=0, tiled=True)  37.2 us
    all_to_all x2, blocking collectives, deliver(): lax.all_to_all(buffer.reshape(experts, 1, slots, width), 'expert', split_...  30.7 us
    dot_general x1, matrix products, body(): jnp.einsum('erd,edf->erf', gathered, w_up, preferred_element_type=jnp.flo...  14.6 us
    all_to_all x2, waiting for transfers between devices, give_back(): lax.all_to_all(rounded, 'expert', split_axis=1, concat_axis=0, tiled=True)  12.8 us
  transfers between devices with their start and end apart: 6, of which 6 were waited for; matrix products, arithmetic and copies ran while one was open for 4% of the time, Pallas kernels for 0%

commit v1 on v0

--- a/solution.py
+++ b/solution.py
@@ -20,8 +20,16 @@
 
 def deliver(buffer, experts, slots):
     width = buffer.shape[-1]
-    sent = lax.all_to_all(
-        buffer.reshape(experts, 1, slots, width), "expert", split_axis=0, concat_axis=1, tiled=True
+    sent = jnp.concatenate(
+        lax.all_to_all(
+            jnp.stack(
+                jnp.split(buffer.reshape(experts, 1, slots, width), lax.axis_size("expert"), axis=0)
+            ),
+            "expert",
+            0,
+            0,
+        ),
+        axis=1,
     )
     shaped = sent.reshape(sent.shape[0], 1, sent.shape[1], slots, width)
     whole = lax.all_gather(shaped, "dp", axis=1, tiled=True)

time: 470 us -> 474 us (level)
  local copies, waits for them, and re-layouts: 34.9 us -> 40.1 us
    unnamed x20 -> x34, local copies, waits for them, and re-layouts: 2.91 us -> 9.33 us
where the time goes in v1:
time: 474 us; the launch traced here: 473 us
  waiting for transfers between devices  190 us (40%)
  blocking collectives  146 us (31%)
  matrix products  50.6 us (11%)
  local copies, waits for them, and re-layouts  40.1 us (8%)
  between operations  19.4 us (4%)
  other arithmetic  18 us (4%)
  starting transfers between devices  8.79 us (2%)
    all_gather x2, waiting for transfers between devices, deliver(): whole = lax.all_gather(shaped, 'dp', axis=1, tiled=True)  95.9 us
    reduce_scatter x2, waiting for transfers between devices, give_back(): lax.psum_scatter(partial_value.reshape(local, n_dp, n_expert * slots, wid...  81.4 us
    psum x1, blocking collectives, body(): lax.psum((loss_term, router_part, gain_partial_term), ('dp', 'expert'))  40.1 us
    all_gather x1, blocking collectives, body(): lax.all_gather(v, ('dp', 'expert'), axis=0, tiled=True)  38.6 us
    all_gather x1, blocking collectives, body(): lax.all_gather(u, ('dp', 'expert'), axis=0, tiled=True)  37.2 us
    all_to_all x2, blocking collectives, deliver(): lax.all_to_all(jnp.stack(jnp.split(buffer.reshape(experts, 1, slots, widt...  30 us
    dot_general x1, matrix products, body(): jnp.einsum('erd,edf->erf', gathered, w_up, preferred_element_type=jnp.flo...  14.6 us
    all_to_all x2, waiting for transfers between devices, give_back(): lax.all_to_all(rounded, 'expert', split_axis=1, concat_axis=0, tiled=True)  12.8 us
  transfers between devices with their start and end apart: 6, of which 6 were waited for; matrix products, arithmetic and copies ran while one was open for 4% of the time, Pallas kernels for 0%

profile of v1, /device:TPU:0, one launch (start us, length us, event | category | flops | bytes accessed | tf_op | source)
XLA Modules:
  0.0 472.9 jit_solution(8388979983942288712)
XLA Ops:
  15.3 16.1 %all_to_all.28 = bf16[8,1,1,36,1024]{4,3,2,1,0:T(8,128)(2,1)S(1)} all-to-all(bf16[8,1,1,36,1024]{4,3,2,1,0:T(8,128)(2,1)S(1)} %fusion.75), channel_id=1, replica_groups=mesh['dp'=4,'expert'=8] {'expert'}, dimensions={0} | all-to-all | bytes 1179648 | tf_op jit(solution)/shard_map/all_to_all | solution.py:24
  32.7 49.5 %all-gather.7.cloned.1.call-done = bf16[32,1,1,36,1024]{4,0,3,2,1:T(8,128)(2,1)} async-done(((bf16[8,1,1,36,1024]{4,0,3,2,1:T(8,128)(2,1)}), bf16[32,1,1,36,1024]{4,0,3,2,1:T(8,128)(2,1)}) %all-gather.7.cloned.1.call-update) | async-done | bytes 2359312 | tf_op jit(solution)/shard_map/all_gather | solution.py:35
  82.1 4.5 copy.35
  86.6 4.1 reshape.528
  90.7 14.6 %fusion.2 = (bf16[1152,1024]{1,0:T(8,128)(2,1)S(1)}, f32[1152,1024]{1,0:T(8,128)}) fusion(bf16[1152,1024]{1,0:T(8,128)(2,1)} %reshape.528, bf16[1,1024,1024]{2,1,0:T(8,128)(2,1)S(1)} %copy-done), kind=kOutput, calls=%fused_computation.9 | convolution fusion | flops 2492596224 | bytes 11534336 | tf_op jit(solution)/shard_map/erd,edf->erf/dot_general | solution.py:84
  106.8 3.8 convert_bitcast_fusion.1
  111.6 45.7 %reduce-scatter.3.cloned.1.call-done = bf16[1,1,288,1024]{3,2,1,0:T(8,128)(2,1)} async-done(((bf16[1,4,288,1024]{3,2,1,0:T(8,128)(2,1)}), bf16[1,1,288,1024]{3,2,1,0:T(8,128)(2,1)}) %reduce-scatter.3.cloned.1.call-update) | async-done | bytes 589840 | tf_op jit(solution)/shard_map/reduce_scatter | solution.py:42
  159.3 4.2 all-to-all-start.1
  165.4 9.2 %all-to-all-done.1 = bf16[1,8,36,1024]{3,2,0,1:T(8,128)(2,1)} async-done(((bf16[1,8,36,1024]{3,2,0,1:T(8,128)(2,1)}), bf16[1,8,36,1024]{3,2,0,1:T(8,128)(2,1)}, u32[]{:S(2)}, u32[]{:S(2)}) %all-to-all-start.1) | async-done | bytes 589856 | tf_op jit(solution)/shard_map/all_to_all | solution.py:49
  181.6 38.6 %all-gather.1 = f32[32768]{0:T(1024)S(1)} all-gather(f32[1024]{0:T(1024)S(1)} %broadcast_divide_fusion), channel_id=3, replica_groups=mesh['dp'=4,'expert'=8] {'dp','expert'}, dimensions={0}, use_global_device_ids=true | all-gather | bytes 135168 | tf_op jit(solution)/shard_map/all_gather | solution.py:109
  220.3 37.2 %all-gather.2 = f32[32768]{0:T(1024)S(1)} all-gather(f32[1024]{0:T(1024)S(1)} %multiply_divide_fusion), channel_id=4, replica_groups=mesh['dp'=4,'expert'=8] {'dp','expert'}, dimensions={0}, use_global_device_ids=true | all-gather | bytes 135168 | tf_op jit(solution)/shard_map/all_gather | solution.py:108
  271.3 13.9 %all_to_all.29 = bf16[8,1,1,36,1024]{4,3,2,1,0:T(8,128)(2,1)S(1)} all-to-all(bf16[8,1,1,36,1024]{4,3,2,1,0:T(8,128)(2,1)S(1)} %fusion.67), channel_id=1, replica_groups=mesh['dp'=4,'expert'=8] {'expert'}, dimensions={0} | all-to-all | bytes 1179648 | tf_op jit(solution)/shard_map/all_to_all | solution.py:24
  286.4 46.4 %all-gather.9.cloned.1.call-done = bf16[32,1,1,36,1024]{4,0,3,2,1:T(8,128)(2,1)} async-done(((bf16[8,1,1,36,1024]{4,0,3,2,1:T(8,128)(2,1)}), bf16[32,1,1,36,1024]{4,0,3,2,1:T(8,128)(2,1)}) %all-gather.9.cloned.1.call-update) | async-done | bytes 2359312 | tf_op jit(solution)/shard_map/all_gather | solution.py:35
  332.8 4.5 copy.38
  337.3 4.1 reshape.535
  341.4 6.9 %fusion.14 = bf16[1152,1024]{1,0:T(8,128)(2,1)S(1)} fusion(f32[1152,1024]{1,0:T(8,128)} %get-tuple-element.13, bf16[1152,1024]{1,0:T(8,128)(2,1)} %reshape.535, bf16[1,1024,1024]{2,1,0:T(8,128)(2,1)} %param.15), kind=kOutput, calls=%fused_computation.29 | convolution fusion | flops 2427715584 | bytes 11534336 | tf_op jit(solution)/shard_map/erd,efd->erf/dot_general | solution.py:131
  349.7 3.9 convert_bitcast_fusion
  356.8 7.7 %convolution_bitcast_fusion = f32[1,1024,1024]{2,1,0:T(8,128)} fusion(bf16[1152,1024]{1,0:T(8,128)(2,1)} %copy-done.8, bf16[1152,1024]{1,0:T(8,128)(2,1)} %reshape.535), kind=kOutput, calls=%fused_computation.32 | convolution fusion | flops 2415919104 | bytes 8912896 | tf_op jit(solution)/shard_map/erf,erd->efd/dot_general | solution.py:133
  364.5 35.7 %reduce-scatter.5.cloned.1.call-done = bf16[1,1,288,1024]{3,2,1,0:T(8,128)(2,1)} async-done(((bf16[1,4,288,1024]{3,2,1,0:T(8,128)(2,1)}), bf16[1,1,288,1024]{3,2,1,0:T(8,128)(2,1)}) %reduce-scatter.5.cloned.1.call-update) | async-done | bytes 589840 | tf_op jit(solution)/shard_map/reduce_scatter | solution.py:42
  402.2 4.4 all-to-all-start.3
  406.7 7.3 %convolution_bitcast_fusion.1 = f32[1,1024,1024]{2,1,0:T(8,128)} fusion(bf16[1152,1024]{1,0:T(8,128)(2,1)} %reshape.528, bf16[1152,1024]{1,0:T(8,128)(2,1)} %copy-done.9), kind=kOutput, calls=%fused_computation.33 | convolution fusion | flops 2415919104 | bytes 8912896 | tf_op jit(solution)/shard_map/erd,erf->edf/dot_general | solution.py:134
  414.0 3.6 all-to-all-done.3
  420.6 3.1 fusion.56
  423.7 40.1 %all-reduce.1 = (f32[1]{0:T(128)}, f32[1024,8]{0,1:T(8,128)}, f32[1024]{0:T(1024)}) all-reduce(f32[1]{0:T(128)} %bitcast.29, f32[1024,8]{0,1:T(8,128)S(1)} %fusion.86, f32[1024]{0:T(1024)S(1)} %get-tuple-element.6), channel_id=1, replica_groups=mesh['dp'=4,'expert'=8] {'dp','expert'}, use_global_device_ids=true, to_apply=%region_13.14 | all-reduce | flops 9217 | bytes 73736 | tf_op jit(solution)/shard_map/psum | solution.py:148
  (96 shorter events, 44.4 us)
Async XLA Ops:
  7.2 83.6 %copy-start = (bf16[1,1024,1024]{2,1,0:T(8,128)(2,1)S(1)}, bf16[1,1024,1024]{2,1,0:T(8,128)(2,1)}, u32[]{:S(2)}) copy-start(bf16[1,1024,1024]{2,1,0:T(8,128)(2,1)} %param.14) | copy-start | bytes 6291460
  7.2 74.9 %all-gather.7.cloned.1.call-start = ((), (), s32[]{:S(2)}) async-start(), calls=%async_computation.8 | async-start | bytes 2949120 | tf_op jit(solution)/shard_map/all_gather | solution.py:35
  32.6 124.6 %reduce-scatter.3.cloned.1.call-start = ((), (), s32[]{:S(2)}) async-start(), calls=%async_computation.6 | async-start | bytes 2949120 | tf_op jit(solution)/shard_map/reduce_scatter | solution.py:42
  90.7 16.1 %copy-start.7 = (bf16[1,1024,1024]{2,1,0:T(8,128)(2,1)S(1)}, bf16[1,1024,1024]{2,1,0:T(8,128)(2,1)}, u32[]{:S(2)}) copy-start(bf16[1,1024,1024]{2,1,0:T(8,128)(2,1)} %param.15) | copy-start | bytes 6291460
  105.3 1.5 copy-start.8
  106.8 4.5 copy-start.1
  106.8 4.5 copy-start.4
  110.6 54.2 %copy-start.5 = (f32[1024,8]{0,1:T(8,128)S(1)}, f32[1024,8]{0,1:T(8,128)}, u32[]{:S(2)}) copy-start(f32[1024,8]{0,1:T(8,128)} %param.13) | copy-start | bytes 98308
  110.6 54.2 %copy-start.6 = (s32[1,212,1]{1,2,0:T(1,128)S(1)}, s32[1,212,1]{1,2,0:T(1,128)}, u32[]{:S(2)}) copy-start(s32[1,212,1]{1,2,0:T(1,128)} %param.10) | copy-start | bytes 2548
  111.6 53.8 %copy-start.3 = (bf16[212,1024]{1,0:T(8,128)(2,1)}, bf16[212,1024]{1,0:T(8,128)(2,1)S(1)}, u32[]{:S(2)}) copy-start(bf16[212,1024]{1,0:T(8,128)(2,1)S(1)} %fusion.50) | copy-start | bytes 1302532
  159.3 15.3 %all-to-all-start.1 = ((bf16[1,8,36,1024]{3,2,0,1:T(8,128)(2,1)}), bf16[1,8,36,1024]{3,2,0,1:T(8,128)(2,1)}, u32[]{:S(2)}, u32[]{:S(2)}) async-start(bf16[1,8,36,1024]{3,2,0,1:T(8,128)(2,1)} %bitcast.246), calls=%async_computation.2 | async-start | bytes 1310720 | tf_op jit(solution)/shard_map/all_to_all | solution.py:49
  163.5 169.3 %all-gather.9.cloned.1.call-start = ((), (), s32[]{:S(2)}) async-start(), calls=%async_computation.9 | async-start | bytes 2949120 | tf_op jit(solution)/shard_map/all_gather | solution.py:35
  261.7 92.6 %copy-start.2 = (f32[1,196,1024]{2,1,0:T(8,128)}, f32[1,196,1024]{2,1,0:T(8,128)S(1)}, u32[]{:S(2)}) copy-start(f32[1,196,1024]{2,1,0:T(8,128)S(1)} %broadcast_in_dim.10) | copy-start | bytes 2408452
  286.4 113.9 %reduce-scatter.5.cloned.1.call-start = ((), (), s32[]{:S(2)}) async-start(), calls=%async_computation.7 | async-start | bytes 2949120 | tf_op jit(solution)/shard_map/reduce_scatter | solution.py:42
  348.2 1.4 copy-start.9
  402.2 15.3 %all-to-all-start.3 = ((bf16[1,8,36,1024]{3,2,0,1:T(8,128)(2,1)}), bf16[1,8,36,1024]{3,2,0,1:T(8,128)(2,1)}, u32[]{:S(2)}, u32[]{:S(2)}) async-start(bf16[1,8,36,1024]{3,2,0,1:T(8,128)(2,1)} %bitcast.48), calls=%async_computation.5 | async-start | bytes 1310720 | tf_op jit(solution)/shard_map/all_to_all | solution.py:49
Sparse Core Ops, SparseCore 0:
  32.8 49.3 all-gather.6
  110.8 46.4 reduce-scatter.2
  286.5 46.2 all-gather.8
  353.7 46.4 reduce-scatter.4
